TPU v7x, 32 devices: a whole 2x2x4 slice. The times are simulated.
32 devices in a mesh: gx: 4 (over y, x), gy: 2 (over core), gz: 4 (over z).
Axes of the slice: x: 2, y: 2, z: 4, core: 2. Of those that a mesh axis runs over, the one named last changes fastest.
Arguments:
- energy: float32 [128, 256, 256], P(('gz', 'gy', 'gx')), may hold values from -5 to 5
- flow: float32 [4, 128, 256, 256], P(None, ('gz', 'gy', 'gx')), may hold values from -0.1 to 0.12, as said below
Outputs:
- energy_next: float32 [128, 256, 256], P('gz', 'gx', 'gy')
- plane_mean: float32 [128], P('gz')
- running_mean: float32 [128], P('gz')
Inputs may be any that keep to these rules, and one draw needn't show every extreme that they name: flow[0], flow[1] and flow[2] lie within -0.1 to 0.1; flow[3] lies within 0.02 to 0.12.
All inputs are finite; a program needn't handle non-finite values.
Results may differ from a plain program's by a relative error of at most 0.00002.
Values sent between devices are 32-bit elements; how exact they have to be, the bound alone decides.
A program may use at most 128 MiB of HBM per device.

v0:
```python
import jax
import jax.numpy as jnp
from jax import lax
from jax.sharding import PartitionSpec as P

directions = ((1, 0, 0), (0, 1, 0), (0, 0, 1))


def padded_2(x, sides, width, wrap):
    for axis, dim in sides:
        size, length = (lax.axis_size(axis), x.shape[dim])
        up = [(i, (i + 1) % size) for i in range(size if wrap else size - 1)]
        down = [(j, i) for i, j in up]
        last = lax.slice_in_dim(x, length - width, length, axis=dim)
        first = lax.slice_in_dim(x, 0, width, axis=dim)
        before = lax.ppermute(last, axis, up)
        after = lax.ppermute(first, axis, down)
        x = jnp.concatenate([before, x, after], axis=dim)
    return x


def entering(value, axis, join, neutral):
    count, mine = (lax.axis_size(axis), lax.axis_index(axis))
    pieces = lax.all_gather(value, axis)
    subtotal = jnp.full_like(value, 0) + jnp.asarray(neutral, value.dtype)

    def hop(position, subtotal):
        longer = join(subtotal, pieces[position])
        return jnp.where(position < mine, longer, subtotal)

    return lax.fori_loop(0, count - 1, hop, subtotal)


def window(array, offset):
    return array[
        1 + offset[0] : array.shape[0] - 1 + offset[0],
        1 + offset[1] : array.shape[1] - 1 + offset[1],
        1 + offset[2] : array.shape[2] - 1 + offset[2],
    ]


def advance(energy_pad, kappa_pad, velocity):
    centre = window(energy_pad, (0, 0, 0))
    kappa_centre = window(kappa_pad, (0, 0, 0))
    change = jnp.zeros_like(centre)
    for axis_number, forward in enumerate(directions):
        backward = tuple((-item for item in forward))
        upper = window(energy_pad, forward)
        lower = window(energy_pad, backward)
        kappa_upper = window(kappa_pad, forward)
        kappa_lower = window(kappa_pad, backward)
        change = (
            change
            + 0.5 * (kappa_centre + kappa_upper) * (upper - centre)
            - 0.5 * (kappa_centre + kappa_lower) * (centre - lower)
        )
        speed = velocity[axis_number]
        change = (
            change
            - jnp.maximum(speed, 0.0) * (centre - lower)
            - jnp.minimum(speed, 0.0) * (upper - centre)
        )
    return centre + change


def fill_planes(stack):
    return padded_2(stack, (("gz", 1),), 1, True)


def fill_all(stack):
    sided = padded_2(stack, (("gx", 2), ("gy", 3)), 1, False)
    return fill_planes(sided)


def add_totals(earlier, later):
    return earlier + later


def per_device(energy, flow):
    pair = jnp.stack([energy, flow[3]])
    padded = jnp.pad(pair, ((0, 0), (0, 0), (1, 1), (1, 1)))
    x_count = lax.axis_size("gx")
    x_width = energy.shape[1] // x_count
    x_pieces = jnp.concatenate(
        [padded[:, :, block * x_width : block * x_width + x_width + 2] for block in range(x_count)],
        2,
    )
    y_count = lax.axis_size("gy")
    y_width = energy.shape[2] // y_count
    y_pieces = jnp.concatenate(
        [
            x_pieces[:, :, :, block * y_width : block * y_width + y_width + 2]
            for block in range(y_count)
        ],
        3,
    )
    extended, velocity = (
        lax.all_to_all(
            lax.all_to_all(y_pieces, "gx", split_axis=2, concat_axis=1, tiled=True),
            "gy",
            split_axis=3,
            concat_axis=1,
            tiled=True,
        ),
        lax.all_to_all(
            lax.all_to_all(flow[:3], "gx", split_axis=2, concat_axis=1, tiled=True),
            "gy",
            split_axis=3,
            concat_axis=1,
            tiled=True,
        ),
    )
    pair_pad = fill_planes(extended)
    kappa_pad = pair_pad[1]
    energy_half = advance(pair_pad[0], kappa_pad, velocity)
    half_pad = fill_all(energy_half[None])[0]
    energy_next = advance(half_pad, kappa_pad, velocity)
    local_sums = jnp.sum(energy_next, axis=(1, 2))
    plane_sums = lax.psum(local_sums, ("gx", "gy"))
    cell_count = (
        energy_next.shape[1] * lax.axis_size("gx") * energy_next.shape[2] * lax.axis_size("gy")
    )
    plane_mean = plane_sums / cell_count
    block_total = jnp.sum(plane_mean)
    position = lax.axis_index("gz")
    offset = entering(block_total, "gz", add_totals, jnp.float32(0.0))
    planes_here = plane_mean.shape[0]
    ranks = (position * planes_here + jnp.arange(planes_here) + 1).astype(jnp.float32)
    running_mean = (offset + jnp.cumsum(plane_mean)) / ranks
    return (energy_next, plane_mean, running_mean)


def solution(mesh):
    placed = (P(("gz", "gy", "gx"), None, None), P(None, ("gz", "gy", "gx"), None, None))
    return jax.shard_map(
        per_device,
        mesh=mesh,
        in_specs=placed,
        out_specs=(P("gz", "gx", "gy"), P("gz"), P("gz")),
        check_vma=False,
    )
```

profile of v0, /device:TPU:0, one launch (start us, length us, event | category | flops | bytes accessed | tf_op | source)
XLA Modules:
  0.0 253.5 jit_solution(12060101802627535595)
XLA Ops:
  0.6 1.4 slice.139
  3.4 3.1 %select_maximum_fusion = f32[2,4,258,258]{3,1,0,2:T(4,128)S(1)} fusion(f32[1,4,256,256]{3,1,0,2:T(4,128)S(1)} %copy.158, f32[1,4,256,256]{3,1,0,2:T(4,128)S(1)} %bitcast.139), kind=kLoop, calls=%fused_computation.7 | loop fusion | flops 6390144 | bytes 4227200 | tf_op jit(solution)/shard_map/stack | solution.py:80
  8.7 3.1 %pad_maximum_fusion.2 = f32[2,4,264,260]{3,1,0,2:T(4,128)} fusion(f32[2,4,264,130]{3,1,0,2:T(4,128)S(1)} %get-tuple-element.111, f32[2,4,264,130]{3,1,0,2:T(4,128)S(1)} %get-tuple-element.110), kind=kLoop, calls=%fused_computation.6 | loop fusion | flops 549120 | bytes 4392960 | tf_op jit(solution)/shard_map/concatenate | solution.py:90
  11.8 5.2 %all-to-all-start = ((f32[2,4,264,260]{3,1,0,2:T(4,128)}), f32[2,4,264,260]{3,1,0,2:T(4,128)S(1)}, u32[]{:S(2)}, u32[]{:S(2)}) async-start(f32[2,4,264,260]{3,1,0,2:T(4,128)} %pad_maximum_fusion.2), calls=%async_computation | async-start | bytes 6488064 | tf_op jit(solution)/shard_map/all_to_all | solution.py:99
  17.0 1.9 slice-done
  18.9 3.7 %copy.159 = f32[3,4,256,256]{3,1,0,2:T(4,128)} copy(f32[3,4,256,256]{3,2,1,0:T(8,128)S(1)} %slice-done) | data formatting | bytes 6291456
  22.5 31.6 %all-to-all-done = f32[2,4,264,260]{3,1,0,2:T(4,128)S(1)} async-done(((f32[2,4,264,260]{3,1,0,2:T(4,128)}), f32[2,4,264,260]{3,1,0,2:T(4,128)S(1)}, u32[]{:S(2)}, u32[]{:S(2)}) %all-to-all-start) | async-done | bytes 2196512 | tf_op jit(solution)/shard_map/all_to_all | solution.py:99
  54.1 1.7 copy-done.1
  55.8 3.6 %copy.131 = f32[2,4,4,66,260]{4,0,3,2,1:T(2,128)S(1)} copy(f32[2,4,4,66,260]{4,2,0,3,1:T(4,128)} %bitcast.135) | data formatting | bytes 4392960 | tf_op jit(solution)/shard_map/all_to_all | solution.py:99
  59.4 5.2 %copy.132 = f32[2,16,66,260]{2,1,0,3:T(8,128)} copy(f32[2,16,66,260]{3,0,2,1:T(2,128)S(1)} %bitcast.134) | data formatting | bytes 4392960 | tf_op jit(solution)/shard_map/all_to_all | solution.py:99
  64.6 12.0 %all_to_all.69 = f32[2,16,66,260]{2,1,0,3:T(8,128)} all-to-all(f32[2,16,66,260]{2,1,0,3:T(8,128)} %copy.132), channel_id=1, replica_groups=mesh['gx'=4,'gy'=2,'gz'=4] {'gy'}, dimensions={3} | all-to-all | bytes 4392960 | tf_op jit(solution)/shard_map/all_to_all | solution.py:98
  76.7 4.9 %all-to-all-start.2 = ((f32[3,4,256,256]{3,1,0,2:T(4,128)}), f32[3,4,256,256]{3,1,0,2:T(4,128)}, u32[]{:S(2)}, u32[]{:S(2)}) async-start(f32[3,4,256,256]{3,1,0,2:T(4,128)} %copy.159), calls=%async_computation.2 | async-start | bytes 6291456 | tf_op jit(solution)/shard_map/all_to_all | solution.py:106
  81.6 9.0 %copy.154 = f32[2,16,66,2,130]{4,3,1,2,0:T(2,128)} copy(f32[2,16,66,2,130]{2,1,0,4,3:T(8,128)} %bitcast.133) | data formatting | bytes 4392960 | tf_op jit(solution)/shard_map/all_to_all | solution.py:98
  90.5 4.7 %copy.155 = f32[2,2,16,66,130]{4,3,2,1,0:T(8,128)S(1)} copy(f32[2,2,16,66,130]{4,1,2,3,0:T(2,128)} %bitcast.128) | data formatting | bytes 4392960 | tf_op jit(solution)/shard_map/all_to_all | solution.py:98
  95.3 1.9 collective-permute-start
  97.2 2.1 collective-permute-start.1
  99.3 4.7 %collective-permute-done = f32[2,1,66,130]{3,2,1,0:T(8,128)S(1)} collective-permute-done((f32[2,1,66,130]{3,2,1,0:T(8,128)S(1)}, f32[2,1,66,130]{3,2,1,0:T(8,128)S(1)}, u32[]{:S(2)}, u32[]{:S(2)}) %collective-permute-start) | collective-permute-done | bytes 68672 | tf_op jit(solution)/shard_map/ppermute | solution.py:16
  104.0 2.0 collective-permute-done.1
  106.4 1.8 slice_bitcast_fusion
  108.2 10.0 %all-to-all-done.2 = f32[3,4,256,256]{3,1,0,2:T(4,128)} async-done(((f32[3,4,256,256]{3,1,0,2:T(4,128)}), f32[3,4,256,256]{3,1,0,2:T(4,128)}, u32[]{:S(2)}, u32[]{:S(2)}) %all-to-all-start.2) | async-done | bytes 3145760 | tf_op jit(solution)/shard_map/all_to_all | solution.py:106
  118.1 2.4 copy.139
  120.6 2.0 copy.140
  122.6 6.9 %copy.141 = f32[3,16,64,256]{2,1,0,3:T(8,128)} copy(f32[3,16,64,256]{3,2,1,0:T(8,128)} %bitcast.137) | data formatting | bytes 6291456 | tf_op jit(solution)/shard_map/all_to_all | solution.py:106
  129.5 6.9 %reshape.57 = f32[2,1,393216]{2,1,0:T(1,128)} reshape(f32[256,3,16,64]{3,2,1,0:T(8,128)} %bitcast.124) | data formatting | bytes 6291456
  136.4 10.4 %all_to_all.70 = f32[2,1,393216]{2,1,0:T(1,128)} all-to-all(f32[2,1,393216]{2,1,0:T(1,128)} %reshape.57), channel_id=1, replica_groups=mesh['gx'=4,'gy'=2,'gz'=4] {'gy'}, dimensions={0} | all-to-all | bytes 6291456 | tf_op jit(solution)/shard_map/all_to_all | solution.py:105
  147.3 12.6 %reduce.2 = f32[2,393216]{1,0:T(2,128)} reduce(f32[2,1,393216]{2,1,0:T(1,128)} %all_to_all.70, f32[]{:T(128)} %broadcast.74), dimensions={1}, to_apply=%all_to_all.62.reduce_sub_computation | reduce | bytes 6291460 | tf_op jit(solution)/shard_map/all_to_all | solution.py:105
  159.8 8.0 %reshape.58 = f32[256,3,16,64]{3,2,1,0:T(8,128)} reshape(f32[2,393216]{1,0:T(2,128)} %reduce.2) | data formatting | bytes 6291456
  167.8 6.4 %copy.143 = f32[3,16,64,2,128]{4,2,1,3,0:T(8,128)} copy(f32[3,16,64,2,128]{2,1,0,4,3:T(8,128)} %bitcast.125) | data formatting | bytes 6291456 | tf_op jit(solution)/shard_map/all_to_all | solution.py:105
  174.3 2.8 %slice_maximum_fusion.2 = (f32[1,2,16,64,128]{4,3,2,1,0:T(8,128)S(1)}, f32[1,2,16,64,128]{4,3,2,1,0:T(8,128)S(1)}, f32[1,2,16,64,128]{4,3,2,1,0:T(8,128)S(1)}, f...) fusion(f32[3,2,16,64,128]{4,3,2,1,0:T(8,128)} %bitcast.138), kind=kLoop, calls=%fused_computation.79 | loop fusion | flops 1572864 | bytes 9437184 | tf_op jit(solution)/shard_map/max | solution.py:60
  177.1 4.3 %fusion.10 = f32[32,64,128]{2,1,0:T(8,128)S(1)} fusion(f32[1,2,16,64,128]{4,3,2,1,0:T(8,128)S(1)} %get-tuple-element.119, f32[1,2,16,64,128]{4,3,2,1,0:T(8,128)S(1)} %get-tuple-element.120, f32[1,2,16,64,128]{4,3,2,1,0:T(8,128)S(1)} %get-tuple-element.118, f32[1,2,16,64,128]{4,3,2,1,0:T(8,128)S(1)} %get-tuple-element.121, ...), kind=kLoop, calls=%fused_computation.42 | loop fusion | flops 11010048 | bytes 22020096 | tf_op jit(solution)/shard_map/add | solution.py:63
  181.5 3.3 %collective-permute-start.2 = (f32[1,32,1,128]{3,1,2,0:T(8,128)S(1)}, f32[1,32,1,128]{3,1,2,0:T(8,128)S(1)}, u32[]{:S(2)}, u32[]{:S(2)}) collective-permute-start(f32[1,32,1,128]{3,1,2,0:T(8,128)S(1)} %bitcast.147), channel_id=1, source_target_pairs={{0,8},{8,16},{16,24},{1,9},{9,17},{17,25},{2,10},{10,18},{18,26},{... | collective-permute-start | bytes 49160 | tf_op jit(solution)/shard_map/ppermute | solution.py:16
  186.3 4.2 %collective-permute-done.3 = f32[1,32,1,128]{3,1,2,0:T(8,128)S(1)} collective-permute-done((f32[1,32,1,128]{3,1,2,0:T(8,128)S(1)}, f32[1,32,1,128]{3,1,2,0:T(8,128)S(1)}, u32[]{:S(2)}, u32[]{:S(2)}) %collective-permute-start.3) | collective-permute-done | bytes 16416 | tf_op jit(solution)/shard_map/ppermute | solution.py:17
  191.2 1.8 fusion.37
  193.0 2.3 copy.148
  195.3 1.9 collective-permute-start.4
  197.2 2.3 copy.149
  200.8 2.2 copy.150
  203.0 2.2 copy.151
  205.2 1.6 pad_maximum_fusion.8
  206.9 1.8 collective-permute-start.6
  208.7 2.1 collective-permute-start.7
  213.5 2.2 collective-permute-done.7
  215.6 2.8 %maximum_bitcast_fusion = f32[34,66,130]{2,1,0:T(8,128)S(1)} fusion(f32[1,1,66,130]{3,2,1,0:T(8,128)} %collective-permute-done.7, f32[1,32,66,1]{3,2,1,0:T(8,128)} %copy.151, f32[1,32,1,128]{3,2,1,0:T(1,128)} %bitcast.145, f32[1,32,64,128]{3,2,1,0:T(8,128)S(1)} %bitcast.132, f32[1,32,1,128]{3,2,1,0:T(1,128)} %bitcast.142, f32[1,32,66,1]{3,2,1,0:T(8,128)} %copy.150, ...), kind=kLoop, calls=%fused_computation.13 | loop fusion | flops 1750320 | bytes 2333760 | tf_op jit(solution)/shard_map/squeeze | solution.py:116
  218.5 6.1 %fusion.32 = (f32[32]{0:T(128)S(1)}, f32[32,64,128]{2,1,0:T(8,128)}) fusion(f32[1,2,16,64,128]{4,3,2,1,0:T(8,128)S(1)} %copy-done.9, f32[1,2,16,64,128]{4,3,2,1,0:T(8,128)S(1)} %copy-done.11, f32[34,66,130]{2,1,0:T(8,128)S(1)} %maximum_bitcast_fusion, f32[34,66,130]{2,1,0:T(8,128)S(1)} %get-tuple-element.104, f32[1,2,16,64,128]{4,3,2,1,0:T(8,128)S(1)} %copy-done.7, ...), kind=kLoop, calls=%fused_computation.89 | loop fusion | flops 11272160 | bytes 22020224 | tf_op jit(solution)/shard_map/reduce_sum | solution.py:118
  224.6 11.9 %psum.7 = f32[32]{0:T(128)S(1)} all-reduce(f32[32]{0:T(128)S(1)} %get-tuple-element.102), channel_id=1, replica_groups=mesh['gx'=4,'gy'=2,'gz'=4] {'gx','gy'}, use_global_device_ids=true, to_apply=%region_1.2 | all-reduce | flops 32 | bytes 256 | tf_op jit(solution)/shard_map/psum | solution.py:119
  237.2 1.4 dynamic-update-slice
  238.6 10.5 %all-reduce.1 = f32[4]{0:T(128)S(1)} all-reduce(f32[4]{0:T(128)S(1)} %dynamic-update-slice), channel_id=1, replica_groups=mesh['gx'=4,'gy'=2,'gz'=4] {'gz'}, use_global_device_ids=true, to_apply=%add.1 | all-reduce | flops 4 | bytes 32
  249.1 3.8 %while.13 = (s32[]{:T(128)}, f32[]{:T(128)}, s32[]{:T(128)}, f32[4]{0:T(128)S(1)}, s32[]{:T(128)}) while((s32[]{:T(128)}, f32[]{:T(128)}, s32[]{:T(128)}, f32[4]{0:T(128)S(1)}, s32[]{:T(128)}) %tuple.51), condition=%wide.region_4.5_spmd, body=%wide.region_3.4_spmd.sunk | while | flops 5 | bytes 107 | solution.py:31
  (60 shorter events, 13.7 us)
Async XLA Ops:
  0.6 2.1 copy-start.13
  11.8 42.4 %all-to-all-start = ((f32[2,4,264,260]{3,1,0,2:T(4,128)}), f32[2,4,264,260]{3,1,0,2:T(4,128)S(1)}, u32[]{:S(2)}, u32[]{:S(2)}) async-start(f32[2,4,264,260]{3,1,0,2:T(4,128)} %pad_maximum_fusion.2), calls=%async_computation | async-start | bytes 6488064 | tf_op jit(solution)/shard_map/all_to_all | solution.py:99
  17.0 1.9 slice-start
  54.1 1.7 copy-start.1
  76.7 41.5 %all-to-all-start.2 = ((f32[3,4,256,256]{3,1,0,2:T(4,128)}), f32[3,4,256,256]{3,1,0,2:T(4,128)}, u32[]{:S(2)}, u32[]{:S(2)}) async-start(f32[3,4,256,256]{3,1,0,2:T(4,128)} %copy.159), calls=%async_computation.2 | async-start | bytes 6291456 | tf_op jit(solution)/shard_map/all_to_all | solution.py:106
  95.3 8.6 %collective-permute-start = (f32[2,1,66,130]{3,2,1,0:T(8,128)S(1)}, f32[2,1,66,130]{3,2,1,0:T(8,128)S(1)}, u32[]{:S(2)}, u32[]{:S(2)}) collective-permute-start(f32[2,1,66,130]{3,2,1,0:T(8,128)S(1)} %get-tuple-element.106), channel_id=1, source_target_pairs={{0,1},{1,2},{2,3},{3,0},{4,5},{5,6},{6,7},{7,4},{8,9},{9,10},{10,1... | collective-permute-start | bytes 205928 | tf_op jit(solution)/shard_map/ppermute | solution.py:16
  97.2 8.8 %collective-permute-start.1 = (f32[2,1,66,130]{3,2,1,0:T(8,128)S(1)}, f32[2,1,66,130]{3,2,1,0:T(8,128)S(1)}, u32[]{:S(2)}, u32[]{:S(2)}) collective-permute-start(f32[2,1,66,130]{3,2,1,0:T(8,128)S(1)} %get-tuple-element.107), channel_id=1, source_target_pairs={{1,0},{2,1},{3,2},{0,3},{5,4},{6,5},{7,6},{4,7},{9,8},{10,9},{11,1... | collective-permute-start | bytes 205928 | tf_op jit(solution)/shard_map/ppermute | solution.py:17
  174.3 2.9 %copy-start = (f32[34,66,130]{2,1,0:T(8,128)S(1)}, f32[34,66,130]{2,1,0:T(8,128)}, u32[]{:S(2)}) copy-start(f32[34,66,130]{2,1,0:T(8,128)} %get-tuple-element.105) | copy-start | bytes 3500644
  177.1 4.4 %copy-start.2 = (f32[1,2,16,64,128]{4,3,2,1,0:T(8,128)}, f32[1,2,16,64,128]{4,3,2,1,0:T(8,128)S(1)}, u32[]{:S(2)}) copy-start(f32[1,2,16,64,128]{4,3,2,1,0:T(8,128)S(1)} %get-tuple-element.116) | copy-start | bytes 3145732
  177.1 4.4 %copy-start.4 = (f32[1,2,16,64,128]{4,3,2,1,0:T(8,128)}, f32[1,2,16,64,128]{4,3,2,1,0:T(8,128)S(1)}, u32[]{:S(2)}) copy-start(f32[1,2,16,64,128]{4,3,2,1,0:T(8,128)S(1)} %get-tuple-element.117) | copy-start | bytes 3145732
  177.1 4.4 %copy-start.6 = (f32[1,2,16,64,128]{4,3,2,1,0:T(8,128)}, f32[1,2,16,64,128]{4,3,2,1,0:T(8,128)S(1)}, u32[]{:S(2)}) copy-start(f32[1,2,16,64,128]{4,3,2,1,0:T(8,128)S(1)} %get-tuple-element.118) | copy-start | bytes 3145732
  177.1 4.4 %copy-start.8 = (f32[1,2,16,64,128]{4,3,2,1,0:T(8,128)}, f32[1,2,16,64,128]{4,3,2,1,0:T(8,128)S(1)}, u32[]{:S(2)}) copy-start(f32[1,2,16,64,128]{4,3,2,1,0:T(8,128)S(1)} %get-tuple-element.119) | copy-start | bytes 3145732
  177.1 4.4 %copy-start.10 = (f32[1,2,16,64,128]{4,3,2,1,0:T(8,128)}, f32[1,2,16,64,128]{4,3,2,1,0:T(8,128)S(1)}, u32[]{:S(2)}) copy-start(f32[1,2,16,64,128]{4,3,2,1,0:T(8,128)S(1)} %get-tuple-element.120) | copy-start | bytes 3145732
  177.1 4.4 %copy-start.12 = (f32[1,2,16,64,128]{4,3,2,1,0:T(8,128)}, f32[1,2,16,64,128]{4,3,2,1,0:T(8,128)S(1)}, u32[]{:S(2)}) copy-start(f32[1,2,16,64,128]{4,3,2,1,0:T(8,128)S(1)} %get-tuple-element.121) | copy-start | bytes 3145732
  181.5 4.8 %collective-permute-start.2 = (f32[1,32,1,128]{3,1,2,0:T(8,128)S(1)}, f32[1,32,1,128]{3,1,2,0:T(8,128)S(1)}, u32[]{:S(2)}, u32[]{:S(2)}) collective-permute-start(f32[1,32,1,128]{3,1,2,0:T(8,128)S(1)} %bitcast.147), channel_id=1, source_target_pairs={{0,8},{8,16},{16,24},{1,9},{9,17},{17,25},{2,10},{10,18},{18,26},{... | collective-permute-start | bytes 49160 | tf_op jit(solution)/shard_map/ppermute | solution.py:16
  184.8 5.6 %collective-permute-start.3 = (f32[1,32,1,128]{3,1,2,0:T(8,128)S(1)}, f32[1,32,1,128]{3,1,2,0:T(8,128)S(1)}, u32[]{:S(2)}, u32[]{:S(2)}) collective-permute-start(f32[1,32,1,128]{3,1,2,0:T(8,128)S(1)} %bitcast.146), channel_id=1, source_target_pairs={{8,0},{16,8},{24,16},{9,1},{17,9},{25,17},{10,2},{18,10},{26,18},{... | collective-permute-start | bytes 49160 | tf_op jit(solution)/shard_map/ppermute | solution.py:17
  186.3 4.2 %copy-start.14 = (f32[1,32,1,128]{3,1,2,0:T(8,128)}, f32[1,32,1,128]{3,1,2,0:T(8,128)S(1)}, u32[]{:S(2)}) copy-start(f32[1,32,1,128]{3,1,2,0:T(8,128)S(1)} %collective-permute-done.2) | copy-start | bytes 49156
  190.5 0.6 copy-start.15
  195.3 5.5 %collective-permute-start.4 = (f32[1,32,66,1]{2,1,3,0:T(8,128)}, f32[1,32,66,1]{2,1,3,0:T(8,128)}, u32[]{:S(2)}, u32[]{:S(2)}) collective-permute-start(f32[1,32,66,1]{2,1,3,0:T(8,128)} %copy.148), channel_id=1, source_target_pairs={{0,4},{1,5},{2,6},{3,7},{8,12},{9,13},{10,14},{11,15},{16,20},{17,... | collective-permute-start | bytes 25352 | tf_op jit(solution)/shard_map/ppermute | solution.py:16
  199.5 3.5 %collective-permute-start.5 = (f32[1,32,66,1]{2,1,3,0:T(8,128)}, f32[1,32,66,1]{2,1,3,0:T(8,128)}, u32[]{:S(2)}, u32[]{:S(2)}) collective-permute-start(f32[1,32,66,1]{2,1,3,0:T(8,128)} %copy.149), channel_id=1, source_target_pairs={{4,0},{5,1},{6,2},{7,3},{12,8},{13,9},{14,10},{15,11},{20,16},{21,... | collective-permute-start | bytes 25352 | tf_op jit(solution)/shard_map/ppermute | solution.py:17
  206.9 6.6 %collective-permute-start.6 = (f32[1,1,66,130]{3,2,1,0:T(8,128)}, f32[1,1,66,130]{3,2,1,0:T(8,128)}, u32[]{:S(2)}, u32[]{:S(2)}) collective-permute-start(f32[1,1,66,130]{3,2,1,0:T(8,128)} %get-tuple-element.108), channel_id=1, source_target_pairs={{0,1},{1,2},{2,3},{3,0},{4,5},{5,6},{6,7},{7,4},{8,9},{9,10},{10,1... | collective-permute-start | bytes 102968 | tf_op jit(solution)/shard_map/ppermute | solution.py:16
  208.7 6.9 %collective-permute-start.7 = (f32[1,1,66,130]{3,2,1,0:T(8,128)}, f32[1,1,66,130]{3,2,1,0:T(8,128)}, u32[]{:S(2)}, u32[]{:S(2)}) collective-permute-start(f32[1,1,66,130]{3,2,1,0:T(8,128)} %get-tuple-element.109), channel_id=1, source_target_pairs={{1,0},{2,1},{3,2},{0,3},{5,4},{6,5},{7,6},{4,7},{9,8},{10,9},{11,1... | collective-permute-start | bytes 102968 | tf_op jit(solution)/shard_map/ppermute | solution.py:17
  212.1 6.3 %copy-start.3 = (f32[1,2,16,64,128]{4,3,2,1,0:T(8,128)S(1)}, f32[1,2,16,64,128]{4,3,2,1,0:T(8,128)}, u32[]{:S(2)}) copy-start(f32[1,2,16,64,128]{4,3,2,1,0:T(8,128)} %copy-done.2) | copy-start | bytes 3145732
  212.1 6.3 %copy-start.5 = (f32[1,2,16,64,128]{4,3,2,1,0:T(8,128)S(1)}, f32[1,2,16,64,128]{4,3,2,1,0:T(8,128)}, u32[]{:S(2)}) copy-start(f32[1,2,16,64,128]{4,3,2,1,0:T(8,128)} %copy-done.4) | copy-start | bytes 3145732
  212.1 6.3 %copy-start.7 = (f32[1,2,16,64,128]{4,3,2,1,0:T(8,128)S(1)}, f32[1,2,16,64,128]{4,3,2,1,0:T(8,128)}, u32[]{:S(2)}) copy-start(f32[1,2,16,64,128]{4,3,2,1,0:T(8,128)} %copy-done.6) | copy-start | bytes 3145732
  212.1 6.3 %copy-start.9 = (f32[1,2,16,64,128]{4,3,2,1,0:T(8,128)S(1)}, f32[1,2,16,64,128]{4,3,2,1,0:T(8,128)}, u32[]{:S(2)}) copy-start(f32[1,2,16,64,128]{4,3,2,1,0:T(8,128)} %copy-done.8) | copy-start | bytes 3145732
  212.1 6.3 %copy-start.11 = (f32[1,2,16,64,128]{4,3,2,1,0:T(8,128)S(1)}, f32[1,2,16,64,128]{4,3,2,1,0:T(8,128)}, u32[]{:S(2)}) copy-start(f32[1,2,16,64,128]{4,3,2,1,0:T(8,128)} %copy-done.10) | copy-start | bytes 3145732
  237.1 16.5 %copy-start.16 = (f32[32]{0:T(128)}, f32[32]{0:T(128)S(1)}, u32[]{:S(2)}) copy-start(f32[32]{0:T(128)S(1)} %get-tuple-element.101) | copy-start | bytes 388
where the time goes:
time: 256 us; the launch traced here: 254 us
  local copies, waits for them, and re-layouts  84.8 us (33%)
  waiting for transfers between devices  56.1 us (22%)
  blocking collectives  44.8 us (18%)
  other arithmetic  39.1 us (15%)
  starting transfers between devices  25.8 us (10%)
    all_to_all x1, waiting for transfers between devices, per_device(): lax.all_to_all(y_pieces, 'gx', split_axis=2, concat_axis=1, tiled=True)  31.6 us
    unnamed x42, local copies, waits for them, and re-layouts  25 us
    all_to_all x2, local copies, waits for them, and re-layouts, per_device(): lax.all_to_all(lax.all_to_all(y_pieces, 'gx', split_axis=2, concat_axis=1...  13.7 us
    all_to_all x1, other arithmetic, per_device(): lax.all_to_all(lax.all_to_all(flow[:3], 'gx', split_axis=2, concat_axis=1...  12.6 us
    all_to_all x1, blocking collectives, per_device(): lax.all_to_all(lax.all_to_all(y_pieces, 'gx', split_axis=2, concat_axis=1...  12 us
    psum x1, blocking collectives, per_device(): plane_sums = lax.psum(local_sums, ('gx', 'gy'))  11.9 us
    all_to_all x3, local copies, waits for them, and re-layouts, per_device(): lax.all_to_all(flow[:3], 'gx', split_axis=2, concat_axis=1, tiled=True)  11.3 us
    unnamed x1, blocking collectives  10.5 us
  transfers between devices with their start and end apart: 10, of which 8 were waited for; matrix products, arithmetic and copies ran while one was open for 10% of the time, Pallas kernels for 0%

commit v1 on v0

v1 whole, which is shorter than its diff:
```python
import functools

import jax
import jax.numpy as jnp
from jax import lax
from jax.experimental import pallas as pl
from jax.experimental.pallas import tpu as pltpu
from jax.sharding import PartitionSpec as P

MESH = pl.DeviceIdType.MESH
PAD = 8
ROWS = 16
STRIP = 32


def shifted(block, rows):
    size = block.shape[0]
    return (
        block[PAD : PAD + rows],
        pltpu.roll(block, size - 1, 0)[PAD : PAD + rows],
        pltpu.roll(block, 1, 0)[PAD : PAD + rows],
    )


def sideways(block, lane):
    width = block.shape[1]
    right = jnp.where(lane == width - 1, 0.0, pltpu.roll(block, width - 1, 1))
    left = jnp.where(lane == 0, 0.0, pltpu.roll(block, 1, 1))
    return right, left


def above(k, k_up, speed, e, e_up):
    return (0.5 * (k + k_up) - jnp.minimum(speed, 0.0)) * (e_up - e)


def below(k, k_down, speed, e, e_down):
    return (0.5 * (k + k_down) + jnp.maximum(speed, 0.0)) * (e_down - e)


def kernel(
    sizes, e_hbm, f_hbm, out, mean_ref, run_ref,
    e_v, k_v, u_v, h_v, n_v, group_v, block_v,
    load_sem, s1, r1, s2, r2, s3, r3, own_sem, s4, r4, s5, r5,
):
    gx_n, gy_n, gz_n, planes, nx, ny = sizes
    height, width = nx // gx_n, ny // gy_n
    gx, gy, gz = lax.axis_index("gx"), lax.axis_index("gy"), lax.axis_index("gz")
    peers = gx_n * gy_n
    place = gy * gx_n + gx
    slab = gz * peers + place

    def device(number):
        return {
            "gx": lax.rem(number, gx_n),
            "gy": lax.rem(lax.div(number, gx_n), gy_n),
            "gz": lax.div(number, peers),
        }

    total = peers * gz_n
    up = device(lax.rem(slab + 1, total))
    down = device(lax.rem(slab + total - 1, total))

    def peer(step):
        return {
            "gx": lax.rem(place + step, gx_n) if gy_n == 1 else lax.rem(lax.rem(place + step, peers), gx_n),
            "gy": lax.div(lax.rem(place + step, peers), gx_n),
            "gz": gz,
        }

    def layer(step):
        return {"gx": gx, "gy": gy, "gz": lax.rem(gz + step, gz_n)}

    loads = [
        pltpu.make_async_copy(e_hbm, e_v.at[pl.ds(1, planes), pl.ds(PAD, nx)], load_sem.at[0]),
        pltpu.make_async_copy(f_hbm.at[3], k_v.at[pl.ds(1, planes), pl.ds(PAD, nx)], load_sem.at[1]),
        pltpu.make_async_copy(f_hbm.at[pl.ds(0, 3)], u_v, load_sem.at[2]),
    ]

    barrier = pltpu.get_barrier_semaphore()
    greet = [up, down] + [peer(i) for i in range(1, peers)] + [layer(i) for i in range(1, gz_n)]
    for target in greet:
        pl.semaphore_signal(barrier, inc=1, device_id=target, device_id_type=MESH)
    for load in loads:
        load.start()
    edge = jnp.zeros((planes, PAD, ny), jnp.float32)
    for ref in (e_v, k_v, h_v):
        ref[1 : planes + 1, 0:PAD, :] = edge
        ref[1 : planes + 1, PAD + nx : PAD + nx + PAD, :] = edge
    pl.semaphore_wait(barrier, len(greet))

    def lanes(c):
        return pl.ds(c * width, width)

    def send(src, dst, send_sem, recv_sem, target):
        return pltpu.make_async_remote_copy(
            src_ref=src, dst_ref=dst, send_sem=send_sem, recv_sem=recv_sem,
            device_id=target, device_id_type=MESH,
        )

    first = []
    rows_all = pl.ds(PAD, nx)
    for c in range(gy_n):
        copies = [
            send(e_hbm.at[planes - 1, :, lanes(c)], e_v.at[0, rows_all, lanes(c)], s1.at[c, 0], r1.at[c, 0], up),
            send(e_hbm.at[0, :, lanes(c)], e_v.at[planes + 1, rows_all, lanes(c)], s1.at[c, 1], r1.at[c, 1], down),
            send(f_hbm.at[3, planes - 1, :, lanes(c)], k_v.at[0, rows_all, lanes(c)], s1.at[c, 2], r1.at[c, 2], up),
            send(f_hbm.at[3, 0, :, lanes(c)], k_v.at[planes + 1, rows_all, lanes(c)], s1.at[c, 3], r1.at[c, 3], down),
        ]
        for copy in copies:
            copy.start()
        first.append(copies)

    for load in loads:
        load.wait()

    lane = lax.broadcasted_iota(jnp.int32, (ROWS, ny), 1)

    def local(src, p, r):
        start = pl.multiple_of(r * ROWS, ROWS)
        here = pl.ds(start, ROWS)
        inner = pl.ds(pl.multiple_of(start + PAD, PAD), ROWS)
        tall = pl.ds(start, ROWS + 2 * PAD)
        e, e_next, e_prev = shifted(src[p + 1, tall, :], ROWS)
        k, k_next, k_prev = shifted(k_v[p + 1, tall, :], ROWS)
        speed = u_v[1, p, here, :]
        value = e + above(k, k_next, speed, e, e_next) + below(k, k_prev, speed, e, e_prev)
        e_next, e_prev = sideways(e, lane)
        k_next, k_prev = sideways(k, lane)
        speed = u_v[2, p, here, :]
        value = value + above(k, k_next, speed, e, e_next) + below(k, k_prev, speed, e, e_prev)
        speed = u_v[0, p, here, :]
        if p < planes - 1:
            value = value + above(k, k_v[p + 2, inner, :], speed, e, src[p + 2, inner, :])
        if p > 0:
            value = value + below(k, k_v[p, inner, :], speed, e, src[p, inner, :])
        return here, inner, value

    def edge_terms(src, c, r):
        start = pl.multiple_of(r * STRIP, STRIP)
        here = pl.ds(start, STRIP)
        inner = pl.ds(pl.multiple_of(start + PAD, PAD), STRIP)
        at = lanes(c)
        top = above(
            k_v[planes, inner, at], k_v[planes + 1, inner, at], u_v[0, planes - 1, here, at],
            src[planes, inner, at], src[planes + 1, inner, at],
        )
        bottom = below(
            k_v[1, inner, at], k_v[0, inner, at], u_v[0, 0, here, at], src[1, inner, at], src[0, inner, at]
        )
        return here, inner, top, bottom

    def folded(value):
        rows = value.shape[0]
        part = value[0:8]
        for i in range(8, rows, 8):
            part = part + value[i : i + 8]
        return part

    for p in range(planes):

        @pl.loop(0, nx // ROWS)
        def _(r, p=p):
            here, inner, value = local(e_v, p, r)
            h_v[p + 1, inner, :] = value

    second = []
    for c in range(gy_n):
        for copy in first[c]:
            copy.wait_recv()

        @pl.loop(0, nx // STRIP)
        def _(r, c=c):
            here, inner, top, bottom = edge_terms(e_v, c, r)
            h_v[planes, inner, lanes(c)] = h_v[planes, inner, lanes(c)] + top
            h_v[1, inner, lanes(c)] = h_v[1, inner, lanes(c)] + bottom

        copies = [
            send(h_v.at[planes, rows_all, lanes(c)], h_v.at[0, rows_all, lanes(c)], s2.at[c, 0], r2.at[c, 0], up),
            send(h_v.at[1, rows_all, lanes(c)], h_v.at[planes + 1, rows_all, lanes(c)], s2.at[c, 1], r2.at[c, 1], down),
        ]
        for copy in copies:
            copy.start()
        second.append(copies)

    sums = []
    for p in range(planes):

        def body(r, carry, p=p):
            here, inner, value = local(h_v, p, r)
            n_v[p, here, :] = value
            return carry + folded(value)

        sums.append(lax.fori_loop(0, nx // ROWS, body, jnp.zeros((8, ny), jnp.float32)))

    def hand_out(c, p0, count, part):
        for d in range(gx_n):
            to = lax.rem(gx + d, gx_n)
            src = n_v.at[pl.ds(p0, count), pl.ds(pl.multiple_of(to * height, 8), height), lanes(c)]
            dst = out.at[pl.ds(place * planes + p0, count)]
            if d == 0:

                @pl.when(gy == c)
                def _():
                    pltpu.make_async_copy(src, dst, own_sem.at[part]).start()

                @pl.when(gy != c)
                def _():
                    send(src, dst, s3.at[c * gx_n + d, part], r3.at[place, part],
                         {"gx": gx, "gy": jnp.int32(c), "gz": gz}).start()
            else:
                send(src, dst, s3.at[c * gx_n + d, part], r3.at[place, part],
                     {"gx": to, "gy": jnp.int32(c), "gz": gz}).start()

    parts = []
    if planes > 2:
        parts.append((1, planes - 2))
        for c in range(gy_n):
            hand_out(c, 1, planes - 2, 0)
    outer = sorted({0, planes - 1})
    first_outer = len(parts)
    parts += [(p, 1) for p in outer]

    extra = [jnp.zeros((8, width), jnp.float32), jnp.zeros((8, width), jnp.float32)]
    for c in range(gy_n):
        for copy in second[c]:
            copy.wait_recv()

        def body(r, carry, c=c):
            here, inner, top, bottom = edge_terms(h_v, c, r)
            n_v[planes - 1, here, lanes(c)] = n_v[planes - 1, here, lanes(c)] + top
            n_v[0, here, lanes(c)] = n_v[0, here, lanes(c)] + bottom
            return carry[0] + folded(top), carry[1] + folded(bottom)

        extra = lax.fori_loop(0, nx // STRIP, body, tuple(extra))
        for part, p in enumerate(outer):
            hand_out(c, p, 1, first_outer + part)

    spot = lax.broadcasted_iota(jnp.int32, (8, 128), 1)
    mine = jnp.zeros((8, 128), jnp.float32)
    for p in range(planes):
        amount = jnp.sum(sums[p], keepdims=True)
        if p == planes - 1:
            amount = amount + jnp.sum(extra[0], keepdims=True)
        if p == 0:
            amount = amount + jnp.sum(extra[1], keepdims=True)
        mine = jnp.where(spot == place * planes + p, amount * (1.0 / (nx * ny)), mine)
    group_v[0] = mine
    share = []
    for i in range(1, peers):
        copy = send(group_v.at[0], group_v.at[i], s4.at[i], r4.at[i], peer(i))
        copy.start()
        share.append(copy)
    for copy in share:
        copy.wait_recv()
    means = mine
    for i in range(1, peers):
        means = means + group_v[i]
    block_v[0] = means
    climb = []
    for i in range(1, gz_n):
        copy = send(block_v.at[0], block_v.at[i], s5.at[i], r5.at[i], layer(i))
        copy.start()
        climb.append(copy)
    running = means
    step = 1
    while step < peers * planes:
        running = running + jnp.where(spot >= step, pltpu.roll(running, step, 1), 0.0)
        step *= 2
    mean_ref[...] = means
    for copy in climb:
        copy.wait_recv()
    lower = jnp.zeros((8, 128), jnp.float32)
    for i in range(1, gz_n):
        lower = lower + jnp.where(gz >= i, block_v[i], 0.0)
    offset = jnp.sum(lower[0:1], axis=1, keepdims=True)
    rank = (gz * peers * planes + spot + 1).astype(jnp.float32)
    run_ref[...] = (running + offset) / rank

    for part, (p0, count) in enumerate(parts):
        for d in range(peers):
            source = lax.rem(place + d, peers)
            dst = out.at[pl.ds(source * planes + p0, count)]
            src = n_v.at[pl.ds(p0, count), pl.ds(0, height), pl.ds(0, width)]
            if d == 0:
                pltpu.make_async_copy(src, dst, own_sem.at[part]).wait()
            else:
                send(src, dst, s3.at[0, part], r3.at[source, part], peer(d)).wait_recv()
        for c in range(gy_n):
            for d in range(gx_n):
                copy = send(
                    n_v.at[pl.ds(p0, count), pl.ds(0, height), pl.ds(0, width)],
                    out.at[pl.ds(p0, count)], s3.at[c * gx_n + d, part], r3.at[0, part], up,
                )
                if d == 0:

                    @pl.when(gy != c)
                    def _():
                        copy.wait_send()
                else:
                    copy.wait_send()
    for copies in first + second + [share, climb]:
        for copy in copies:
            copy.wait_send()


def per_device(energy, flow):
    gx_n, gy_n, gz_n = (lax.axis_size(a) for a in ("gx", "gy", "gz"))
    planes, nx, ny = energy.shape
    peers = gx_n * gy_n
    parts = (1 if planes > 2 else 0) + (2 if planes > 1 else 1)
    dma = pltpu.SemaphoreType.DMA
    f32 = jnp.float32
    anywhere = pl.BlockSpec(memory_space=pl.ANY)
    vmem = pl.BlockSpec(memory_space=pltpu.VMEM)
    tall = pltpu.VMEM((planes + 2, nx + 2 * PAD, ny), f32)
    energy_next, means, running = pl.pallas_call(
        functools.partial(kernel, (gx_n, gy_n, gz_n, planes, nx, ny)),
        out_shape=(
            jax.ShapeDtypeStruct((planes * peers, nx // gx_n, ny // gy_n), f32),
            jax.ShapeDtypeStruct((8, 128), f32),
            jax.ShapeDtypeStruct((8, 128), f32),
        ),
        in_specs=[anywhere, anywhere],
        out_specs=(anywhere, vmem, vmem),
        scratch_shapes=[
            tall, tall, pltpu.VMEM((3, planes, nx, ny), f32), tall,
            pltpu.VMEM((planes, nx, ny), f32),
            pltpu.VMEM((peers, 8, 128), f32), pltpu.VMEM((gz_n, 8, 128), f32),
            dma((3,)), dma((gy_n, 4)), dma((gy_n, 4)), dma((gy_n, 2)), dma((gy_n, 2)),
            dma((peers, parts)), dma((peers, parts)), dma((parts,)),
            dma((peers,)), dma((peers,)), dma((gz_n,)), dma((gz_n,)),
        ],
        compiler_params=pltpu.CompilerParams(collective_id=0, has_side_effects=True),
    )(energy, flow)
    count = planes * peers
    return energy_next, means[0, :count], running[0, :count]


def solution(mesh):
    placed = (P(("gz", "gy", "gx"), None, None), P(None, ("gz", "gy", "gx"), None, None))
    return jax.shard_map(
        per_device,
        mesh=mesh,
        in_specs=placed,
        out_specs=(P("gz", "gx", "gy"), P("gz"), P("gz")),
        check_vma=False,
    )
```

time: 256 us -> 62.4 us (0.24)
  local copies, waits for them, and re-layouts: 84.8 us -> 3.5 us
  Pallas kernels: 0 us -> 58 us
  waiting for transfers between devices: 56.1 us -> 0 us
  blocking collectives: 44.8 us -> 0 us
  other arithmetic: 39.1 us -> 0 us
  starting transfers between devices: 25.8 us -> 0 us
    pallas_call x0 -> x1, Pallas kernels: none -> 58 us  [per_device(): pl.pallas_call(functools.partial(kernel, (gx_n, gy_n, gz_n, planes, nx, n...]
    all_to_all x2 -> x0, waiting for transfers between devices: 41.6 us -> none  [the longest x1 31.6 us: per_device(): lax.all_to_all(y_pieces, 'gx', split_axis=2, concat_axis=1, tiled=True)]
    all_to_all x9 -> x0, local copies, waits for them, and re-layouts: 40.8 us -> none  [the longest x2 13.7 us: per_device(): lax.all_to_all(lax.all_to_all(y_pieces, 'gx', split_axis=2, concat_axis=1...]
    unnamed x42 -> x1, local copies, waits for them, and re-layouts: 25 us -> 2.31 us
    all_to_all x2 -> x0, blocking collectives: 22.4 us -> none  [the longest x1 12 us: per_device(): lax.all_to_all(lax.all_to_all(y_pieces, 'gx', split_axis=2, concat_axis=1...]
    ppermute x8 -> x0, starting transfers between devices: 15.7 us -> none  [the longest x4 8.91 us: padded_2(): before = lax.ppermute(last, axis, up)]
    ppermute x8 -> x0, waiting for transfers between devices: 14.5 us -> none  [the longest x4 8.37 us: padded_2(): after = lax.ppermute(first, axis, down)]
    all_to_all x1 -> x0, other arithmetic: 12.6 us -> none  [per_device(): lax.all_to_all(lax.all_to_all(flow[:3], 'gx', split_axis=2, concat_axis=1...]
  transfers between devices with their start and end apart: 10 -> 0, of which waited for: 8 -> 0; matrix products, arithmetic and copies ran while one was open for 10% -> 0% of each run, Pallas kernels for 0% -> 0%
where the time goes in v1:
time: 62.4 us; the launch traced here: 62.2 us
  Pallas kernels  58 us (93%)
  local copies, waits for them, and re-layouts  3.5 us (6%)
  between operations  0.64 us (1%)
    pallas_call x1, Pallas kernels, per_device(): pl.pallas_call(functools.partial(kernel, (gx_n, gy_n, gz_n, planes, nx, n...  58 us
    unnamed x1, local copies, waits for them, and re-layouts  2.31 us

profile of v1, /device:TPU:0, one launch (start us, length us, event | category | flops | bytes accessed | tf_op | source)
XLA Modules:
  0.0 62.2 jit_solution(18266936109167822019)
XLA Ops:
  0.6 58.0 %shard_map.49 = (f32[32,64,128]{2,1,0:T(8,128)}, f32[8,128]{1,0:T(8,128)}, f32[8,128]{1,0:T(8,128)}) custom-call(f32[4,256,256]{2,1,0:T(8,128)} %e_hbm.1, f32[4,4,256,256]{3,2,1,0:T(8,128)} %f_hbm.1), custom_call_target="tpu_custom_call" | custom-call | tf_op jit(solution)/shard_map/pallas_call | solution.py:316
  58.7 1.2 %slice_bitcast_fusion = (f32[32]{0:T(128)}, f32[32]{0:T(128)}) fusion(f32[8,128]{1,0:T(8,128)} %get-tuple-element.8, f32[8,128]{1,0:T(8,128)} %get-tuple-element.7), kind=kLoop, calls=%fused_computation | loop fusion | bytes 512 | tf_op jit(solution)/shard_map/squeeze | solution.py:336
  59.9 2.3 %copy.6 = f32[32,64,128]{2,1,0:T(8,128)} copy(f32[32,64,128]{2,1,0:T(8,128)} %get-tuple-element.14) | data formatting | bytes 2097152

commit v2 on v1

--- a/solution.py
+++ b/solution.py
@@ -303,9 +303,386 @@
             copy.wait_send()
 
 
+def split_kernel(
+    sizes, e_hbm, f_hbm, out, corr, mean_ref, run_ref,
+    e_v, k_v, u_v, h_v, n_v, g_v, rx_v, d_v, c_v, near_v, far_v, group_v, block_v,
+    load_sem, s1, r1, s2, r2, s3, r3, sc, rc, s4, r4, s5, r5,
+):
+    gx_n, gy_n, gz_n, planes, nx, ny = sizes
+    height, width = nx // gx_n, ny // gy_n
+    halves = gx_n // 2
+    gx, gy, gz = lax.axis_index("gx"), lax.axis_index("gy"), lax.axis_index("gz")
+    peers = gx_n * gy_n
+    count = peers * planes
+    place = gy * gx_n + gx
+    slab = gz * peers + place
+    parity = lax.rem(gx, 2)
+    total = peers * gz_n
+    above_slab, below_slab = lax.rem(slab + 1, total), lax.rem(slab + total - 1, total)
+    last = planes - 1
+    own_plane = (0, last)
+
+    def device(number):
+        return {
+            "gx": lax.rem(number, gx_n),
+            "gy": lax.rem(lax.div(number, gx_n), gy_n),
+            "gz": lax.div(number, peers),
+        }
+
+    neighbour = (device(below_slab), device(above_slab))
+
+    def peer(step):
+        return device(gz * peers + lax.rem(place + step, peers))
+
+    def layer(step):
+        return {"gx": gx, "gy": gy, "gz": lax.rem(gz + step, gz_n)}
+
+    loads = [
+        pltpu.make_async_copy(e_hbm, e_v.at[:, pl.ds(PAD, nx)], load_sem.at[0]),
+        pltpu.make_async_copy(f_hbm.at[3], k_v.at[:, pl.ds(PAD, nx)], load_sem.at[1]),
+        pltpu.make_async_copy(f_hbm.at[pl.ds(0, 3)], u_v, load_sem.at[2]),
+    ]
+    for load in loads:
+        load.start()
+
+    barrier = pltpu.get_barrier_semaphore()
+    greet = list(neighbour) + [peer(i) for i in range(1, peers)] + [layer(i) for i in range(1, gz_n)]
+    greet.append(device(lax.rem(gz + gz_n - 1, gz_n) * peers + peers - 1))
+    greet.append(device(lax.rem(gz + 1, gz_n) * peers))
+    for target in greet:
+        pl.semaphore_signal(barrier, inc=1, device_id=target, device_id_type=MESH)
+    edge = jnp.zeros((planes, PAD, ny), jnp.float32)
+    for ref in (e_v, k_v, h_v):
+        ref[:, 0:PAD, :] = edge
+        ref[:, PAD + nx : PAD + nx + PAD, :] = edge
+    outermost = (place == 0).astype(jnp.int32) + (place == peers - 1).astype(jnp.int32)
+    pl.semaphore_wait(barrier, len(greet) - 2 + outermost * peers)
+
+    def lanes(c):
+        return pl.ds(c * width, width)
+
+    def send(src, dst, send_sem, recv_sem, target):
+        return pltpu.make_async_remote_copy(
+            src_ref=src, dst_ref=dst, send_sem=send_sem, recv_sem=recv_sem,
+            device_id=target, device_id_type=MESH,
+        )
+
+    def row(block, extra=0):
+        return pl.multiple_of(block * height + extra, 8)
+
+    mine = [2 * j + parity for j in range(halves)]
+    theirs = [2 * j + 1 - parity for j in range(halves)]
+
+    first = {}
+
+    def start_first(j, fields):
+        for f in (1, 0):
+            p, rows = own_plane[f], pl.ds(row(theirs[j]), height)
+            inner = pl.ds(row(theirs[j], PAD), height)
+            sources = (e_hbm.at[p, rows], f_hbm.at[3, p, rows], g_v.at[f, rows], h_v.at[p, inner])
+            for i in fields:
+                copy = send(sources[i], rx_v.at[1 - f, i, j], s1.at[f, i, j], r1.at[1 - f, i, j], neighbour[f])
+                copy.start()
+                first[f, i, j] = copy
+
+    start_first(0, (0, 1))
+    for load in loads:
+        load.wait()
+
+    lane = lax.broadcasted_iota(jnp.int32, (ROWS, ny), 1)
+    tiles = height // ROWS
+
+    def local(src, p, start):
+        here = pl.ds(start, ROWS)
+        inner = pl.ds(pl.multiple_of(start + PAD, 8), ROWS)
+        tall = pl.ds(start, ROWS + 2 * PAD)
+        e, e_next, e_prev = shifted(src[p, tall, :], ROWS)
+        k, k_next, k_prev = shifted(k_v[p, tall, :], ROWS)
+        speed = u_v[1, p, here, :]
+        value = e + above(k, k_next, speed, e, e_next) + below(k, k_prev, speed, e, e_prev)
+        e_next, e_prev = sideways(e, lane)
+        k_next, k_prev = sideways(k, lane)
+        speed = u_v[2, p, here, :]
+        value = value + above(k, k_next, speed, e, e_next) + below(k, k_prev, speed, e, e_prev)
+        speed = u_v[0, p, here, :]
+        if p < last:
+            value = value + above(k, k_v[p + 1, inner, :], speed, e, src[p + 1, inner, :])
+        if p > 0:
+            value = value + below(k, k_v[p - 1, inner, :], speed, e, src[p - 1, inner, :])
+        return here, inner, value, 0.5 * k, speed
+
+    def folded(value):
+        part = value[0:8]
+        for i in range(8, value.shape[0], 8):
+            part = part + value[i : i + 8]
+        return part
+
+    def first_step(block, which):
+        @pl.loop(0, tiles)
+        def _(t):
+            start = pl.multiple_of(block * height + t * ROWS, 8)
+            for p in which:
+                here, inner, value, half, speed = local(e_v, p, start)
+                h_v[p, inner, :] = value
+                if p == 0:
+                    g_v[0, here, :] = half + jnp.maximum(speed, 0.0)
+                if p == last:
+                    g_v[1, here, :] = half - jnp.minimum(speed, 0.0)
+
+    for j in range(halves):
+        if j > 0:
+            start_first(j, (0, 1))
+        first_step(theirs[j], own_plane)
+        start_first(j, (2, 3))
+    for j in range(halves):
+        first_step(mine[j], own_plane)
+    inside = tuple(range(1, last))
+    if inside:
+        for block in range(gx_n):
+            first_step(block, inside)
+
+    second, fixes = [], []
+    side_slab = (below_slab, above_slab)
+    zero = jnp.zeros((8, ny), jnp.float32)
+    spill = (zero, zero)
+    for j in range(halves):
+        for f in (0, 1):
+            for i in range(4):
+                send(rx_v.at[f, i, j], rx_v.at[f, i, j], s1.at[f, i, j], r1.at[f, i, j], neighbour[f]).wait_recv()
+
+        def body(t, carry, j=j):
+            sums = []
+            at = pl.ds(pl.multiple_of(t * ROWS, 8), ROWS)
+            start = pl.multiple_of(mine[j] * height + t * ROWS, 8)
+            here, inner = pl.ds(start, ROWS), pl.ds(pl.multiple_of(start + PAD, 8), ROWS)
+            for f in (0, 1):
+                p = own_plane[f]
+                to_near = g_v[f, here, :] + 0.5 * rx_v[f, 1, j, at, :]
+                to_far = rx_v[f, 2, j, at, :] + 0.5 * k_v[p, inner, :]
+                step = rx_v[f, 0, j, at, :] - e_v[p, inner, :]
+                push = to_far * step
+                d_v[f, j, at, :] = -push
+                here_half = h_v[p, inner, :] + to_near * step
+                far_half = rx_v[f, 3, j, at, :] - push
+                h_v[p, inner, :] = here_half
+                step = far_half - here_half
+                near_v[f, j, at, :] = to_near * step
+                fix = -(to_far * step)
+                far_v[f, j, at, :] = fix
+                sums.append(carry[f] + folded(fix))
+            return tuple(sums)
+
+        spill = lax.fori_loop(0, tiles, body, spill)
+        for f in (1, 0):
+            copy = send(d_v.at[f, j], c_v.at[1 - f, j], s2.at[f, j], r2.at[1 - f, j], neighbour[f])
+            copy.start()
+            second.append(copy)
+
+    def fix_copies(act):
+        for j in range(halves):
+            for f in (0, 1):
+                far_place, far_block = lax.rem(side_slab[f], peers), lax.div(side_slab[f], peers)
+                slot = lax.div(far_place, 2)
+                for c in range(gy_n):
+                    at_home = (mine[j] == gx) & (gy == c) & (far_block == gz)
+                    act(
+                        at_home, far_v.at[f, j, :, lanes(c)], corr.at[slot, 1 - f], sc.at[f, j, c],
+                        rc.at[slot, 1 - f], {"gx": mine[j], "gy": jnp.int32(c), "gz": far_block},
+                    )
+
+    def begin(at_home, src, dst, send_sem, recv_sem, target):
+        @pl.when(at_home)
+        def _():
+            pltpu.make_async_copy(src, dst, recv_sem).start()
+
+        @pl.when(jnp.logical_not(at_home))
+        def _():
+            send(src, dst, send_sem, recv_sem, target).start()
+
+    def finish(at_home, src, dst, send_sem, recv_sem, target):
+        @pl.when(jnp.logical_not(at_home))
+        def _():
+            send(src, dst, send_sem, recv_sem, target).wait_send()
+
+    fix_copies(begin)
+
+    sums = [zero] * planes
+
+    def second_step(block, j, own):
+        for p in range(planes):
+
+            def body(t, carry, p=p):
+                start = pl.multiple_of(block * height + t * ROWS, 8)
+                at = pl.ds(pl.multiple_of(t * ROWS, 8), ROWS)
+                here, inner, value, half, speed = local(h_v, p, start)
+                for f in (0, 1):
+                    if own and p == own_plane[f]:
+                        value = value + near_v[f, j, at, :]
+                n_v[p, here, :] = value
+                return carry + folded(value)
+
+            sums[p] = lax.fori_loop(0, tiles, body, sums[p])
+
+    def hand_out(block, j, own, act):
+        for c in range(gy_n):
+            at_home = (block == gx) & (gy == c)
+            act(
+                at_home, n_v.at[:, pl.ds(row(block), height), lanes(c)], out.at[pl.ds(place * planes, planes)],
+                s3.at[2 * j + own, c], r3.at[place], {"gx": block, "gy": jnp.int32(c), "gz": gz},
+            )
+
+    for j in range(halves):
+        for f in (0, 1):
+            first[f, 3, j].wait_send()
+            send(d_v.at[f, j], c_v.at[f, j], s2.at[f, j], r2.at[f, j], neighbour[f]).wait_recv()
+
+        @pl.loop(0, tiles)
+        def _(t, j=j):
+            at = pl.ds(pl.multiple_of(t * ROWS, 8), ROWS)
+            inner = pl.ds(pl.multiple_of(theirs[j] * height + t * ROWS + PAD, 8), ROWS)
+            for f in (0, 1):
+                h_v[own_plane[f], inner, :] = h_v[own_plane[f], inner, :] + c_v[f, j, at, :]
+
+        second_step(theirs[j], j, 0)
+        hand_out(theirs[j], j, 0, begin)
+    for j in range(halves):
+        second_step(mine[j], j, 1)
+        hand_out(mine[j], j, 1, begin)
+
+    spot = lax.broadcasted_iota(jnp.int32, (8, 128), 1)
+    scale = 1.0 / (nx * ny)
+    part = jnp.zeros((8, 128), jnp.float32)
+    base = place * planes
+    amounts = [jnp.sum(spill[0], keepdims=True)] + [jnp.sum(s, keepdims=True) for s in sums]
+    amounts.append(jnp.sum(spill[1], keepdims=True))
+    for i, amount in enumerate(amounts):
+        part = jnp.where(spot == base + i, amount * scale, part)
+    group_v[0] = part
+    share = []
+    for i in range(1, peers):
+        copy = send(group_v.at[0], group_v.at[i], s4.at[i], r4.at[i], peer(i))
+        copy.start()
+        share.append(copy)
+    for copy in share:
+        copy.wait_recv()
+    for i in range(1, peers):
+        part = part + group_v[i]
+    block_v[0] = part
+    climb = []
+    for i in range(1, gz_n):
+        copy = send(block_v.at[0], block_v.at[i], s5.at[i], r5.at[i], layer(i))
+        copy.start()
+        climb.append(copy)
+    for copy in climb:
+        copy.wait_recv()
+    lower = jnp.zeros((8, 128), jnp.float32)
+    own_lane = (spot >= 1) & (spot <= count)
+    means = jnp.where(own_lane, part, 0.0)
+    for i in range(gz_n):
+        vector = block_v[i]
+        block = lax.rem(gz + gz_n - i, gz_n)
+        owner = jnp.where(own_lane, block, jnp.where(
+            spot == 0, lax.rem(block + gz_n - 1, gz_n), lax.rem(block + 1, gz_n)))
+        vector = jnp.where(spot <= count + 1, vector, 0.0)
+        lower = lower + jnp.where(owner < gz, vector, 0.0)
+        low = jnp.sum(jnp.where((spot == 0) & (owner == gz), vector, 0.0)[0:1], axis=1, keepdims=True)
+        high = jnp.sum(jnp.where((spot == count + 1) & (owner == gz), vector, 0.0)[0:1], axis=1, keepdims=True)
+        means = means + jnp.where(spot == count, low, 0.0) + jnp.where(spot == 1, high, 0.0)
+    means = pltpu.roll(means, 127, 1)
+    running = means
+    step = 1
+    while step < count:
+        running = running + jnp.where(spot >= step, pltpu.roll(running, step, 1), 0.0)
+        step *= 2
+    mean_ref[...] = means
+    offset = jnp.sum(lower[0:1], axis=1, keepdims=True)
+    rank = (gz * count + spot + 1).astype(jnp.float32)
+    run_ref[...] = (running + offset) / rank
+
+    for s in range(peers):
+        dst = out.at[pl.ds(s * planes, planes)]
+        send(dst, dst, s3.at[0, 0], r3.at[s], neighbour[0]).wait_recv()
+    for slot in range(peers // 2):
+        for f in (0, 1):
+            send(corr.at[slot, f], corr.at[slot, f], sc.at[0, 0, 0], rc.at[slot, f], neighbour[0]).wait_recv()
+    for j in range(halves):
+        hand_out(theirs[j], j, 0, finish)
+        hand_out(mine[j], j, 1, finish)
+    fix_copies(finish)
+    for key, copy in first.items():
+        if key[1] != 3:
+            copy.wait_send()
+    for copy in second + share + climb:
+        copy.wait_send()
+
+
+def finish_kernel(planes, base_ref, corr_ref, mean_in, run_in, out_ref, mean_ref, run_ref):
+    out_ref[...] = base_ref[...]
+    start = (1 - lax.rem(lax.axis_index("gx"), 2)) * planes
+    for f, p in ((0, 0), (1, planes - 1)):
+        out_ref[start + p] = out_ref[start + p] + corr_ref[0, f]
+    count = mean_ref.shape[0]
+    mean_ref[...] = mean_in[0, 0:count]
+    run_ref[...] = run_in[0, 0:count]
+
+
+def by_parity(energy, flow):
+    gx_n, gy_n, gz_n = (lax.axis_size(a) for a in ("gx", "gy", "gz"))
+    planes, nx, ny = energy.shape
+    peers, halves = gx_n * gy_n, gx_n // 2
+    height, width = nx // gx_n, ny // gy_n
+    dma = pltpu.SemaphoreType.DMA
+    f32 = jnp.float32
+    anywhere = pl.BlockSpec(memory_space=pl.ANY)
+    vmem = pl.BlockSpec(memory_space=pltpu.VMEM)
+    tall = pltpu.VMEM((planes, nx + 2 * PAD, ny), f32)
+    faces = pltpu.VMEM((2, halves, height, ny), f32)
+    base, corr, means, running = pl.pallas_call(
+        functools.partial(split_kernel, (gx_n, gy_n, gz_n, planes, nx, ny)),
+        out_shape=(
+            jax.ShapeDtypeStruct((planes * peers, height, width), f32),
+            jax.ShapeDtypeStruct((peers // 2, 2, height, width), f32),
+            jax.ShapeDtypeStruct((8, 128), f32),
+            jax.ShapeDtypeStruct((8, 128), f32),
+        ),
+        in_specs=[anywhere, anywhere],
+        out_specs=(anywhere, anywhere, vmem, vmem),
+        scratch_shapes=[
+            tall, tall, pltpu.VMEM((3, planes, nx, ny), f32), tall,
+            pltpu.VMEM((planes, nx, ny), f32), pltpu.VMEM((2, nx, ny), f32),
+            pltpu.VMEM((2, 4, halves, height, ny), f32), faces, faces, faces, faces,
+            pltpu.VMEM((peers, 8, 128), f32), pltpu.VMEM((gz_n, 8, 128), f32),
+            dma((3,)), dma((2, 4, halves)), dma((2, 4, halves)), dma((2, halves)), dma((2, halves)),
+            dma((gx_n, gy_n)), dma((peers,)), dma((2, halves, gy_n)), dma((peers // 2, 2)),
+            dma((peers,)), dma((peers,)), dma((gz_n,)), dma((gz_n,)),
+        ],
+        compiler_params=pltpu.CompilerParams(collective_id=0, has_side_effects=True),
+    )(energy, flow)
+    steps, count = peers // 2, planes * peers
+    row = pl.BlockSpec((8, 128), lambda i: (0, 0))
+    line = pl.BlockSpec((count,), lambda i: (0,))
+    return tuple(pl.pallas_call(
+        functools.partial(finish_kernel, planes),
+        grid=(steps,),
+        out_shape=(
+            jax.ShapeDtypeStruct((count, height, width), f32),
+            jax.ShapeDtypeStruct((count,), f32),
+            jax.ShapeDtypeStruct((count,), f32),
+        ),
+        in_specs=[
+            pl.BlockSpec((2 * planes, height, width), lambda i: (i, 0, 0)),
+            pl.BlockSpec((1, 2, height, width), lambda i: (i, 0, 0, 0)),
+            row, row,
+        ],
+        out_specs=(pl.BlockSpec((2 * planes, height, width), lambda i: (i, 0, 0)), line, line),
+    )(base, corr, means, running))
+
+
 def per_device(energy, flow):
     gx_n, gy_n, gz_n = (lax.axis_size(a) for a in ("gx", "gy", "gz"))
     planes, nx, ny = energy.shape
+    if planes > 1 and gx_n % 2 == 0 and gz_n > 1:
+        return by_parity(energy, flow)
     peers = gx_n * gy_n
     parts = (1 if planes > 2 else 0) + (2 if planes > 1 else 1)
     dma = pltpu.SemaphoreType.DMA

time: 62.4 us -> 61 us (0.978)
  the two profiles are of different devices: /device:TPU:0 before, /device:TPU:4 now
where the time goes in v2:
time: 61 us; the launch traced here: 60.8 us
  Pallas kernels  60.2 us (99%)
  between operations  0.64 us (1%)
    pallas_call x1, Pallas kernels, by_parity(): pl.pallas_call(functools.partial(split_kernel, (gx_n, gy_n, gz_n, planes,...  56.7 us
    pallas_call x1, Pallas kernels, by_parity(): pl.pallas_call(functools.partial(finish_kernel, planes), grid=(steps,), o...  3.41 us

profile of v2, /device:TPU:4, one launch (start us, length us, event | category | flops | bytes accessed | tf_op | source)
XLA Modules:
  0.0 60.8 jit_solution(14265841628310834826)
XLA Ops:
  0.6 56.7 %shard_map.49 = (f32[32,64,128]{2,1,0:T(8,128)}, f32[4,2,64,128]{3,2,1,0:T(8,128)}, f32[8,128]{1,0:T(8,128)}, f32[8,128]{1,0:T(8,128)}) custom-call(f32[4,256,256]{2,1,0:T(8,128)} %e_hbm.1, f32[4,4,256,256]{3,2,1,0:T(8,128)} %f_hbm.1), custom_call_target="tpu_custom_call" | custom-call | tf_op jit(solution)/shard_map/pallas_call | solution.py:640
  57.4 3.4 %shard_map.50 = (f32[32,64,128]{2,1,0:T(8,128)}, f32[32]{0:T(128)}, f32[32]{0:T(128)}) custom-call(f32[32,64,128]{2,1,0:T(8,128)} %get-tuple-element.7.base_ref, f32[4,2,64,128]{3,2,1,0:T(8,128)} %get-tuple-element.8.corr_ref, f32[8,128]{1,0:T(8,128)} %get-tuple-element.9.mean_in, f32[8,128]{1,0:T(8,128)} %get-tuple-element.10.run_in), custom_call_target="tpu_custom_call" | custom-call | tf_op jit(solution)/shard_map/pallas_call | solution.py:664

commit v3 on v2

--- a/solution.py
+++ b/solution.py
@@ -544,10 +544,10 @@
                 h_v[own_plane[f], inner, :] = h_v[own_plane[f], inner, :] + c_v[f, j, at, :]
 
         second_step(theirs[j], j, 0)
-        hand_out(theirs[j], j, 0, begin)
+        if j < halves - 1:
+            hand_out(theirs[j], j, 0, begin)
     for j in range(halves):
         second_step(mine[j], j, 1)
-        hand_out(mine[j], j, 1, begin)
 
     spot = lax.broadcasted_iota(jnp.int32, (8, 128), 1)
     scale = 1.0 / (nx * ny)
@@ -563,6 +563,9 @@
         copy = send(group_v.at[0], group_v.at[i], s4.at[i], r4.at[i], peer(i))
         copy.start()
         share.append(copy)
+    hand_out(theirs[-1], halves - 1, 0, begin)
+    for j in range(halves):
+        hand_out(mine[j], j, 1, begin)
     for copy in share:
         copy.wait_recv()
     for i in range(1, peers):
@@ -616,14 +619,25 @@
         copy.wait_send()
 
 
-def finish_kernel(planes, base_ref, corr_ref, mean_in, run_in, out_ref, mean_ref, run_ref):
-    out_ref[...] = base_ref[...]
-    start = (1 - lax.rem(lax.axis_index("gx"), 2)) * planes
-    for f, p in ((0, 0), (1, planes - 1)):
-        out_ref[start + p] = out_ref[start + p] + corr_ref[0, f]
+def finish_kernel(planes, base_ref, corr_ref, mean_in, run_in, out_ref, mean_ref, run_ref, fix_v, done):
+    other = 1 - lax.rem(lax.axis_index("gx"), 2)
+    copies = []
+    for slot in range(corr_ref.shape[0]):
+        whole = pl.ds((2 * slot + 1 - other) * planes, planes)
+        copies.append(pltpu.make_async_copy(base_ref.at[whole], out_ref.at[whole], done.at[slot, 0]))
+        copies[-1].start()
+    for slot in range(corr_ref.shape[0]):
+        start = (2 * slot + other) * planes
+        fix_v[slot] = base_ref[pl.ds(start, planes)]
+        for f, p in ((0, 0), (1, planes - 1)):
+            fix_v[slot, p] = fix_v[slot, p] + corr_ref[slot, f]
+        copies.append(pltpu.make_async_copy(fix_v.at[slot], out_ref.at[pl.ds(start, planes)], done.at[slot, 1]))
+        copies[-1].start()
     count = mean_ref.shape[0]
     mean_ref[...] = mean_in[0, 0:count]
     run_ref[...] = run_in[0, 0:count]
+    for copy in copies:
+        copy.wait()
 
 
 def by_parity(energy, flow):
@@ -636,7 +650,9 @@
     anywhere = pl.BlockSpec(memory_space=pl.ANY)
     vmem = pl.BlockSpec(memory_space=pltpu.VMEM)
     tall = pltpu.VMEM((planes, nx + 2 * PAD, ny), f32)
+    hbm = pl.BlockSpec(memory_space=pltpu.HBM)
     faces = pltpu.VMEM((2, halves, height, ny), f32)
+    energy, flow = (pltpu.with_memory_space_constraint(x, pltpu.HBM) for x in (energy, flow))
     base, corr, means, running = pl.pallas_call(
         functools.partial(split_kernel, (gx_n, gy_n, gz_n, planes, nx, ny)),
         out_shape=(
@@ -645,7 +661,7 @@
             jax.ShapeDtypeStruct((8, 128), f32),
             jax.ShapeDtypeStruct((8, 128), f32),
         ),
-        in_specs=[anywhere, anywhere],
+        in_specs=[hbm, hbm],
         out_specs=(anywhere, anywhere, vmem, vmem),
         scratch_shapes=[
             tall, tall, pltpu.VMEM((3, planes, nx, ny), f32), tall,
@@ -656,25 +672,22 @@
             dma((gx_n, gy_n)), dma((peers,)), dma((2, halves, gy_n)), dma((peers // 2, 2)),
             dma((peers,)), dma((peers,)), dma((gz_n,)), dma((gz_n,)),
         ],
-        compiler_params=pltpu.CompilerParams(collective_id=0, has_side_effects=True),
+        compiler_params=pltpu.CompilerParams(
+            collective_id=0, has_side_effects=True, vmem_limit_bytes=8 * (energy.size + flow.size)
+        ),
     )(energy, flow)
-    steps, count = peers // 2, planes * peers
-    row = pl.BlockSpec((8, 128), lambda i: (0, 0))
-    line = pl.BlockSpec((count,), lambda i: (0,))
+    count = planes * peers
     return tuple(pl.pallas_call(
         functools.partial(finish_kernel, planes),
-        grid=(steps,),
         out_shape=(
             jax.ShapeDtypeStruct((count, height, width), f32),
             jax.ShapeDtypeStruct((count,), f32),
             jax.ShapeDtypeStruct((count,), f32),
         ),
-        in_specs=[
-            pl.BlockSpec((2 * planes, height, width), lambda i: (i, 0, 0)),
-            pl.BlockSpec((1, 2, height, width), lambda i: (i, 0, 0, 0)),
-            row, row,
-        ],
-        out_specs=(pl.BlockSpec((2 * planes, height, width), lambda i: (i, 0, 0)), line, line),
+        in_specs=[vmem] * 4,
+        out_specs=(pl.BlockSpec(memory_space=pltpu.HBM), vmem, vmem),
+        scratch_shapes=[pltpu.VMEM((peers // 2, planes, height, width), f32), dma((peers // 2, 2))],
+        compiler_params=pltpu.CompilerParams(vmem_limit_bytes=8 * (energy.size + flow.size)),
     )(base, corr, means, running))
 
 

time: 61 us -> 56.3 us (0.923)
  the two profiles are of different devices: /device:TPU:4 before, /device:TPU:0 now
where the time goes in v3:
time: 56.3 us; the launch traced here: 56.2 us
  Pallas kernels  55.5 us (99%)
  between operations  0.64 us (1%)
    pallas_call x1, Pallas kernels, by_parity(): pl.pallas_call(functools.partial(split_kernel, (gx_n, gy_n, gz_n, planes,...  54 us
    pallas_call x1, Pallas kernels, by_parity(): pl.pallas_call(functools.partial(finish_kernel, planes), out_shape=(jax.S...  1.55 us

profile of v3, /device:TPU:0, one launch (start us, length us, event | category | flops | bytes accessed | tf_op | source)
XLA Modules:
  0.0 56.2 jit_solution(480426922207455220)
XLA Ops:
  0.6 54.0 %shard_map.49 = (f32[32,64,128]{2,1,0:T(8,128)S(1)}, f32[4,2,64,128]{3,2,1,0:T(8,128)S(1)}, f32[8,128]{1,0:T(8,128)S(1)}, f32[8,128]{1,0:T(8,128)S(1)}) custom-call(f32[4,256,256]{2,1,0:T(8,128)} %e_hbm.1, f32[4,4,256,256]{3,2,1,0:T(8,128)} %f_hbm.1), custom_call_target="tpu_custom_call" | custom-call | tf_op jit(solution)/shard_map/pallas_call | solution.py:656
  54.6 1.6 %shard_map.50 = (f32[32,64,128]{2,1,0:T(8,128)}, f32[32]{0:T(128)}, f32[32]{0:T(128)}) custom-call(f32[32,64,128]{2,1,0:T(8,128)S(1)} %get-tuple-element.7.base_ref, f32[4,2,64,128]{3,2,1,0:T(8,128)S(1)} %get-tuple-element.8.corr_ref, f32[8,128]{1,0:T(8,128)S(1)} %get-tuple-element.9.mean_in, f32[8,128]{1,0:T(8,128)S(1)} %get-tuple-element.10.run_in), custom_call_target="tpu_custom_call" | custom-call | tf_op jit(solution)/shard_map/pallas_call | solution.py:680

commit v4 on v3

--- a/solution.py
+++ b/solution.py
@@ -445,6 +445,31 @@
     side_slab = (below_slab, above_slab)
     zero = jnp.zeros((8, ny), jnp.float32)
     spill = (zero, zero)
+    sums = [zero] * planes
+
+    def second_step(block, j, own, p, low, high):
+        def body(t, carry):
+            start = pl.multiple_of(block * height + t * ROWS, 8)
+            at = pl.ds(pl.multiple_of(t * ROWS, 8), ROWS)
+            here, inner, value, half, speed = local(h_v, p, start)
+            for f in (0, 1):
+                if own and p == own_plane[f]:
+                    value = value + near_v[f, j, at, :]
+            n_v[p, here, :] = value
+            return carry + folded(value)
+
+        sums[p] = lax.fori_loop(low, high, body, sums[p])
+
+    def ahead(j):
+        for p in range(planes):
+            inside = 0 < p < last
+            second_step(mine[j], j, 1, p, 0 if inside else 1, tiles if inside else tiles - 1)
+
+    def behind(j):
+        for p in own_plane:
+            for t in sorted({0, tiles - 1}):
+                second_step(mine[j], j, 1, p, t, t + 1)
+
     for j in range(halves):
         for f in (0, 1):
             for i in range(4):
@@ -477,6 +502,8 @@
             copy = send(d_v.at[f, j], c_v.at[1 - f, j], s2.at[f, j], r2.at[1 - f, j], neighbour[f])
             copy.start()
             second.append(copy)
+        if j < halves - 1:
+            ahead(j)
 
     def fix_copies(act):
         for j in range(halves):
@@ -505,23 +532,7 @@
             send(src, dst, send_sem, recv_sem, target).wait_send()
 
     fix_copies(begin)
-
-    sums = [zero] * planes
-
-    def second_step(block, j, own):
-        for p in range(planes):
-
-            def body(t, carry, p=p):
-                start = pl.multiple_of(block * height + t * ROWS, 8)
-                at = pl.ds(pl.multiple_of(t * ROWS, 8), ROWS)
-                here, inner, value, half, speed = local(h_v, p, start)
-                for f in (0, 1):
-                    if own and p == own_plane[f]:
-                        value = value + near_v[f, j, at, :]
-                n_v[p, here, :] = value
-                return carry + folded(value)
-
-            sums[p] = lax.fori_loop(0, tiles, body, sums[p])
+    ahead(halves - 1)
 
     def hand_out(block, j, own, act):
         for c in range(gy_n):
@@ -543,11 +554,12 @@
             for f in (0, 1):
                 h_v[own_plane[f], inner, :] = h_v[own_plane[f], inner, :] + c_v[f, j, at, :]
 
-        second_step(theirs[j], j, 0)
+        for p in range(planes):
+            second_step(theirs[j], j, 0, p, 0, tiles)
         if j < halves - 1:
             hand_out(theirs[j], j, 0, begin)
     for j in range(halves):
-        second_step(mine[j], j, 1)
+        behind(j)
 
     spot = lax.broadcasted_iota(jnp.int32, (8, 128), 1)
     scale = 1.0 / (nx * ny)
@@ -673,7 +685,7 @@
             dma((peers,)), dma((peers,)), dma((gz_n,)), dma((gz_n,)),
         ],
         compiler_params=pltpu.CompilerParams(
-            collective_id=0, has_side_effects=True, vmem_limit_bytes=8 * (energy.size + flow.size)
+            collective_id=0, has_side_effects=True, vmem_limit_bytes=12 * (energy.size + flow.size)
         ),
     )(energy, flow)
     count = planes * peers
@@ -687,7 +699,7 @@
         in_specs=[vmem] * 4,
         out_specs=(pl.BlockSpec(memory_space=pltpu.HBM), vmem, vmem),
         scratch_shapes=[pltpu.VMEM((peers // 2, planes, height, width), f32), dma((peers // 2, 2))],
-        compiler_params=pltpu.CompilerParams(vmem_limit_bytes=8 * (energy.size + flow.size)),
+        compiler_params=pltpu.CompilerParams(vmem_limit_bytes=12 * (energy.size + flow.size)),
     )(base, corr, means, running))
 
 

time: 56.3 us -> 54.1 us (0.961)
  Pallas kernels: 55.5 us -> 53.3 us
    pallas_call x1, Pallas kernels: 54 us -> 51.8 us  [by_parity(): pl.pallas_call(functools.partial(split_kernel, (gx_n, gy_n, gz_n, planes,...]
where the time goes in v4:
time: 54.1 us; the launch traced here: 54 us
  Pallas kernels  53.3 us (99%)
  between operations  0.64 us (1%)
    pallas_call x1, Pallas kernels, by_parity(): pl.pallas_call(functools.partial(split_kernel, (gx_n, gy_n, gz_n, planes,...  51.8 us
    pallas_call x1, Pallas kernels, by_parity(): pl.pallas_call(functools.partial(finish_kernel, planes), out_shape=(jax.S...  1.55 us

profile of v4, /device:TPU:0, one launch (start us, length us, event | category | flops | bytes accessed | tf_op | source)
XLA Modules:
  0.0 54.0 jit_solution(15671510501751161951)
XLA Ops:
  0.6 51.8 %shard_map.49 = (f32[32,64,128]{2,1,0:T(8,128)S(1)}, f32[4,2,64,128]{3,2,1,0:T(8,128)S(1)}, f32[8,128]{1,0:T(8,128)S(1)}, f32[8,128]{1,0:T(8,128)S(1)}) custom-call(f32[4,256,256]{2,1,0:T(8,128)} %e_hbm.1, f32[4,4,256,256]{3,2,1,0:T(8,128)} %f_hbm.1), custom_call_target="tpu_custom_call" | custom-call | tf_op jit(solution)/shard_map/pallas_call | solution.py:668
  52.4 1.6 %shard_map.50 = (f32[32,64,128]{2,1,0:T(8,128)}, f32[32]{0:T(128)}, f32[32]{0:T(128)}) custom-call(f32[32,64,128]{2,1,0:T(8,128)S(1)} %get-tuple-element.7.base_ref, f32[4,2,64,128]{3,2,1,0:T(8,128)S(1)} %get-tuple-element.8.corr_ref, f32[8,128]{1,0:T(8,128)S(1)} %get-tuple-element.9.mean_in, f32[8,128]{1,0:T(8,128)S(1)} %get-tuple-element.10.run_in), custom_call_target="tpu_custom_call" | custom-call | tf_op jit(solution)/shard_map/pallas_call | solution.py:692
